TPU v7x, 32 devices: a whole 2x2x4 slice. The times are simulated.
32 devices in a mesh: lat: 16 (over z, x, core), chan: 2 (over y).
Axes of the slice: x: 2, y: 2, z: 4, core: 2. Of those that a mesh axis runs over, the one named last changes fastest.
Arguments:
- spec_in: bfloat16 [384, 1, 256, 2, 384], P('lat', None, 'chan'), may hold values from -6 to 6
- legendre: float32 [384, 384, 384], P('lat'), may hold values from -0.4375 to 0.4375
- mode_slot: int32 [384], replicated, may hold values from 0 to 383, each once
- w_in: bfloat16 [512, 256], replicated, may hold values from -0.375 to 0.375
- b_in: float32 [512], replicated, may hold values from -3 to 3
- w_out: bfloat16 [256, 512], replicated, may hold values from -0.25 to 0.25
- kernel: float32 [256, 9], P('chan'), may hold values from -4 to 4
Outputs:
- spec_out: bfloat16 [384, 1, 256, 2, 384], P('lat', None, 'chan')
Inputs may be any that keep to these rules, and one draw needn't show every extreme that they name: mode_slot holds every number of 0 to 383 once.
All inputs are finite; a program needn't handle non-finite values.
Results may differ from a plain program's by a relative error of at most 0.0083.
Values may be sent and summed in bfloat16 or wider, within the bound.
A program may use at most 192 MiB of HBM per device.

v0:
```python
import math

import jax
import jax.numpy as jnp
from jax import lax
from jax.sharding import PartitionSpec as P

NLON = 768


def with_halo(array, sides, width):
    for axis, dim in sides:
        count, length = (lax.axis_size(axis), array.shape[dim])
        up = [(i, (i + 1) % count) for i in range(count - 1)]
        down = [(j, i) for i, j in up]
        last = lax.slice_in_dim(array, length - width, length, axis=dim)
        first = lax.slice_in_dim(array, 0, width, axis=dim)
        before = lax.ppermute(last, axis, up)
        after = lax.ppermute(first, axis, down)
        array = jnp.concatenate([before, array, after], axis=dim)
    return array


def wave_table(modes, count):
    columns = jnp.arange(count, dtype=jnp.int32)
    phase = modes[:, None] * columns[None, :] % count
    angle = phase.astype(jnp.float32) * (2.0 * math.pi / count)
    factor = count ** (-0.5)
    return jnp.stack([jnp.cos(angle) * factor, -jnp.sin(angle) * factor], axis=1)


def on_device(spec_in, legendre, mode_slot, w_in, b_in, w_out, kernel):
    high = lax.Precision.HIGHEST
    slots_here = legendre.shape[0]
    lat_index = lax.axis_index("lat")
    local_modes = lax.dynamic_slice_in_dim(mode_slot, lat_index * slots_here, slots_here)
    degrees = jnp.arange(legendre.shape[2], dtype=jnp.int32)
    masked = jnp.where(
        degrees[None, None, :] >= local_modes[:, None, None], legendre, jnp.float32(0.0)
    )
    waves = wave_table(mode_slot, NLON)
    coeff = jnp.einsum("sbcrl,stl->sbcrt", spec_in.astype(jnp.float32), masked, precision=high)
    grid = jnp.einsum(
        "sbcrt,srp->btcp",
        lax.all_to_all(coeff, "lat", split_axis=4, concat_axis=0, tiled=True),
        waves,
        precision=high,
    ).astype(jnp.bfloat16)
    batch, rows_here, chan_here, columns = grid.shape
    whole = lax.all_gather(grid, "chan", axis=2, tiled=True)
    chan_index = lax.axis_index("chan")
    w_local = lax.dynamic_slice_in_dim(w_out, chan_index * chan_here, chan_here, 0)
    pre = jnp.einsum("hc,btcp->bthp", w_in, whole, preferred_element_type=jnp.float32)
    hidden = jax.nn.gelu(pre + b_in[None, None, :, None], approximate=True).astype(jnp.bfloat16)
    branch = jnp.einsum("ch,bthp->btcp", w_local, hidden, preferred_element_type=jnp.float32)
    mixed = (grid.astype(jnp.float32) + branch).astype(jnp.bfloat16)
    half = columns // 2
    last_row = lax.axis_size("lat") - 1
    padded = with_halo(mixed, (("lat", 1),), 1)
    upper = jnp.where(lat_index == 0, jnp.roll(mixed[:, 0:1], half, axis=3), padded[:, 0:1])
    lower = jnp.where(lat_index == last_row, jnp.roll(mixed[:, -1:], half, axis=3), padded[:, -1:])
    stacked = jnp.concatenate([upper, padded[:, 1:-1], lower], axis=1).astype(jnp.float32)
    wide = mixed.astype(jnp.float32)
    conv = jnp.zeros_like(wide)
    for i in range(3):
        band = stacked[:, i : i + rows_here]
        for j in range(3):
            conv = conv + kernel[:, 3 * i + j][None, None, :, None] * jnp.roll(band, 1 - j, axis=3)
    field = wide + conv
    modes = jnp.einsum("btcp,srp->sbcrt", field, waves, precision=high)
    return jnp.einsum(
        "sbcrt,stl->sbcrl",
        lax.all_to_all(modes, "lat", split_axis=0, concat_axis=4, tiled=True),
        masked,
        precision=high,
    ).astype(jnp.bfloat16)


def solution(mesh):
    in_specs = (
        P("lat", None, "chan", None, None),
        P("lat", None, None),
        P(),
        P(),
        P(),
        P(),
        P("chan", None),
    )
    out_specs = P("lat", None, "chan", None, None)
    return jax.shard_map(
        on_device, mesh=mesh, in_specs=in_specs, out_specs=out_specs, check_vma=False
    )
```

profile of v0, /device:TPU:1, one launch (start us, length us, event | category | flops | bytes accessed | tf_op | source)
XLA Modules:
  0.0 785.7 jit_solution(9206927735117521160)
XLA Ops:
  6.5 0.8 dynamic_slice.6
  7.3 0.1 iota_compare_fusion
  7.4 12.3 %fusion.67 = f32[24,1,128,2,384]{2,4,3,0,1:T(8,128)S(1)} fusion(bf16[24,128,2,384]{3,2,1,0:T(2,128)(2,1)} %bitcast.119, f32[24,384,384]{2,1,0:T(8,128)} %param.8, pred[24,384]{1,0:T(8,128)(4,1)S(1)} %iota_compare_fusion), kind=kOutput, calls=%fused_computation.74 | convolution fusion | flops 10875174912 | bytes 28320768 | tf_op jit(solution)/shard_map/sbcrl,stl->sbcrt/dot_general | solution.py:42
  19.8 21.3 %copy.30 = f32[24,1,128,2,384]{2,3,0,1,4:T(2,128)} copy(f32[24,1,128,2,384]{2,4,3,0,1:T(8,128)S(1)} %fusion.67) | data formatting | bytes 18874368 | tf_op jit(solution)/shard_map/sbcrl,stl->sbcrt/dot_general | solution.py:42
  41.1 7.4 all-to-all-start
  48.5 0.0 all-gather.2.cloned.1.call-start
  48.6 4.8 cosine_multiply_fusion
  53.4 164.5 %all-to-all-done = f32[24,1,128,2,384]{2,3,0,1,4:T(2,128)} async-done(((f32[24,1,128,2,384]{2,3,0,1,4:T(2,128)}), f32[24,1,128,2,384]{2,3,0,1,4:T(2,128)}, u32[]{:S(2)}, u32[]{:S(2)}) %all-to-all-start) | async-done | bytes 9437216 | tf_op jit(solution)/shard_map/all_to_all | solution.py:45
  218.0 4.9 copy.31
  222.9 0.0 copy-start.7
  222.9 0.0 copy-start.8
  222.9 24.7 %fusion.53 = bf16[1,24,128,768]{2,3,1,0:T(8,128)(2,1)} fusion(f32[384,128,2,24]{1,0,2,3:T(8,128)S(1)} %bitcast.118, f32[384,1,768]{0,2,1:T(8,128)S(1)} %get-tuple-element.33, f32[384,1,768]{0,2,1:T(8,128)S(1)} %get-tuple-element.32), kind=kOutput, calls=%fused_computation.61 | convolution fusion | flops 21746221056 | bytes 16515072 | tf_op jit(solution)/shard_map/sbcrt,srp->btcp/dot_general | solution.py:43
  247.7 0.0 all-gather.2.cloned.1.call-update
  247.7 152.9 %all-gather.2.cloned.1.call-done = bf16[1,24,256,768]{2,3,1,0:T(8,128)(2,1)} async-done(((bf16[1,24,128,768]{2,3,1,0:T(8,128)(2,1)}), bf16[1,24,256,768]{2,3,1,0:T(8,128)(2,1)}) %all-gather.2.cloned.1.call-update) | async-done | bytes 9437200 | tf_op jit(solution)/shard_map/all_gather | solution.py:50
  400.6 18.7 %fusion.45 = bf16[1,24,128,768]{2,3,1,0:T(8,128)(2,1)} fusion(bf16[1,24,128,768]{2,3,1,0:T(8,128)(2,1)} %fusion.53, f32[512]{0:T(512)S(1)} %copy-done.8, bf16[1,24,256,768]{2,3,1,0:T(8,128)(2,1)} %all-gather.2.cloned.1.call-done, bf16[512,256]{1,0:T(8,128)(2,1)S(1)} %copy-done, bf16[256,512]{1,0:T(8,128)(2,1)S(1)} %copy-done.7, s32[]{:T(128)S(6)} %select_n.45), kind=kOutput, calls=%fused_computation.52 | convolution fusion | flops 7349207040 | bytes 19269636 | tf_op jit(solution)/shard_map/ch,bthp->btcp/dot_general | solution.py:55
  419.3 1.2 fusion.100
  420.5 4.0 collective-permute-start
  424.5 2.1 collective-permute-start.1
  426.6 1.1 fusion.99
  427.6 0.1 maximum_select_fusion
  427.7 3.7 collective-permute-done.1
  431.5 0.1 maximum_select_fusion.1
  431.5 1.1 maximum_convert_fusion.1
  432.6 4.7 maximum_convert_fusion
  437.3 38.6 %fusion.98 = (f32[1,24,128,767]{2,3,1,0:T(8,128)}, f32[1,24,128,767]{2,3,1,0:T(8,128)}, f32[1,24,128,767]{2,3,1,0:T(8,128)}, f32[1,24,128,767]{2,3,1,0:T(8,128)}...) fusion(f32[1,26,128,768]{2,3,1,0:T(8,128)} %maximum_convert_fusion), kind=kLoop, calls=%fused_computation.117 | loop fusion | bytes 113098752 | tf_op jit(solution)/shard_map/jit(_roll_static)/slice | solution.py:68
  475.9 41.4 %fusion.64 = f32[384,1,128,2,24]{2,0,4,3,1:T(8,128)} fusion(f32[1,26,128,768]{2,3,1,0:T(8,128)} %maximum_convert_fusion, f32[1,24,128,767]{2,3,1,0:T(8,128)} %get-tuple-element.9, f32[1,24,128,1]{2,3,1,0:T(1,128)S(1)} %get-tuple-element.16, f32[1,24,128,1]{2,3,1,0:T(1,128)S(1)} %get-tuple-element.15, f32[1,24,128,767]{2,3,1,0:T(8,128)} %get-tuple-element.7, ...), kind=kOutput, calls=%fused_computation.73 | convolution fusion | flops 21802844160 | bytes 101528064 | tf_op jit(solution)/shard_map/btcp,srp->sbcrt/dot_general | solution.py:70
  517.3 9.1 %copy.34 = f32[384,1,128,2,24]{2,4,3,1,0:T(8,128)S(1)} copy(f32[384,1,128,2,24]{2,0,4,3,1:T(8,128)} %fusion.64) | data formatting | bytes 18874368 | tf_op jit(solution)/shard_map/btcp,srp->sbcrt/transpose | solution.py:70
  526.5 0.0 slice-start
  526.5 211.0 %all_to_all.30 = f32[384,1,128,2,24]{2,4,3,1,0:T(8,128)} all-to-all(f32[384,1,128,2,24]{2,4,3,1,0:T(8,128)S(1)} %copy.34), channel_id=1, replica_groups=mesh['lat'=16,'chan'=2] {'lat'}, dimensions={0} | all-to-all | bytes 18874368 | tf_op jit(solution)/shard_map/all_to_all | solution.py:73
  737.5 8.7 %copy.35 = f32[24,1,128,2,16,24]{2,5,4,3,0,1:T(8,128)} copy(f32[24,1,128,2,16,24]{2,5,3,1,0,4:T(8,128)} %bitcast.117) | data formatting | bytes 18874368 | tf_op jit(solution)/shard_map/all_to_all | solution.py:73
  746.3 22.6 %convert_bitcast_fusion = bf16[24,1,128,2,384]{4,2,3,0,1:T(8,128)(2,1)} fusion(f32[24,128,2,384]{1,3,2,0:T(8,128)} %bitcast.116, f32[24,384,384]{2,1,0:T(8,128)S(1)} %bitcast.115, pred[24,384]{1,0:T(8,128)(4,1)S(1)} %copy-done.4), kind=kOutput, calls=%fused_computation.63 | convolution fusion | flops 10877534208 | bytes 28320768 | tf_op jit(solution)/shard_map/sbcrt,stl->sbcrl/dot_general | solution.py:71
  768.9 9.4 %copy.37 = bf16[24,1,128,2,384]{4,3,2,1,0:T(2,128)(2,1)} copy(bf16[24,1,128,2,384]{4,2,3,0,1:T(8,128)(2,1)} %convert_bitcast_fusion) | data formatting | bytes 9437184 | tf_op jit(solution)/shard_map/convert_element_type | solution.py:76
  (26 shorter events, 0.1 us)
Async XLA Ops:
  6.5 394.0 %copy-start = (bf16[512,256]{1,0:T(8,128)(2,1)S(1)}, bf16[512,256]{1,0:T(8,128)(2,1)}, u32[]{:S(2)}) copy-start(bf16[512,256]{1,0:T(8,128)(2,1)} %param.10) | copy-start | bytes 786436
  7.4 12.4 %copy-start.3 = (pred[24,384]{1,0:T(8,128)(4,1)}, pred[24,384]{1,0:T(8,128)(4,1)S(1)}, u32[]{:S(2)}) copy-start(pred[24,384]{1,0:T(8,128)(4,1)S(1)} %iota_compare_fusion) | copy-start | bytes 27652
  41.1 7.5 copy-start.6
  41.1 176.9 %all-to-all-start = ((f32[24,1,128,2,384]{2,3,0,1,4:T(2,128)}), f32[24,1,128,2,384]{2,3,0,1,4:T(2,128)}, u32[]{:S(2)}, u32[]{:S(2)}) async-start(f32[24,1,128,2,384]{2,3,0,1,4:T(2,128)} %copy.30), calls=%async_computation | async-start | bytes 18874368 | tf_op jit(solution)/shard_map/all_to_all | solution.py:45
  48.5 352.0 %all-gather.2.cloned.1.call-start = ((), (), s32[]{:S(2)}) async-start(), calls=%async_computation.2 | async-start | bytes 14155776 | tf_op jit(solution)/shard_map/all_gather | solution.py:50
  222.9 24.8 %copy-start.5 = (f32[128,9]{0,1:T(8,128)S(1)}, f32[128,9]{0,1:T(8,128)}, u32[]{:S(2)}) copy-start(f32[128,9]{0,1:T(8,128)} %param.13) | copy-start | bytes 13828
  222.9 177.7 %copy-start.7 = (bf16[256,512]{1,0:T(8,128)(2,1)S(1)}, bf16[256,512]{1,0:T(8,128)(2,1)}, u32[]{:S(2)}) copy-start(bf16[256,512]{1,0:T(8,128)(2,1)} %param.12) | copy-start | bytes 786436
  222.9 177.6 %copy-start.8 = (f32[512]{0:T(512)S(1)}, f32[512]{0:T(512)}, u32[]{:S(2)}) copy-start(f32[512]{0:T(512)} %param.11) | copy-start | bytes 6148
  419.3 13.3 %copy-start.2 = (bf16[1,24,128,768]{2,3,1,0:T(8,128)(2,1)S(1)}, bf16[1,24,128,768]{2,3,1,0:T(8,128)(2,1)}, u32[]{:S(2)}) copy-start(bf16[1,24,128,768]{2,3,1,0:T(8,128)(2,1)} %fusion.45) | copy-start | bytes 14155780
  420.5 7.1 collective-permute-start
  424.5 7.0 collective-permute-start.1
  526.5 219.8 %slice-start = ((s8[14155776]{0:T(1024)(128)(4,1)}), s8[4194304]{0:T(1024)(128)(4,1)S(1)}, s32[]{:S(2)}) async-start(s8[14155776]{0:T(1024)(128)(4,1)} %bitcast.114), calls=%async_computation.3 | async-start | bytes 8388608
  526.5 219.8 %slice-start.1 = ((s8[14155776]{0:T(1024)(128)(4,1)}), s8[4194304]{0:T(1024)(128)(4,1)S(1)}, s32[]{:S(2)}) async-start(s8[14155776]{0:T(1024)(128)(4,1)} %bitcast.114), calls=%async_computation.4 | async-start | bytes 8388608
  737.5 8.7 %slice-start.2 = ((s8[14155776]{0:T(1024)(128)(4,1)}), s8[4194304]{0:T(1024)(128)(4,1)S(1)}, s32[]{:S(2)}) async-start(s8[14155776]{0:T(1024)(128)(4,1)} %bitcast.114), calls=%async_computation.5 | async-start | bytes 8388608
  737.5 8.7 %slice-start.3 = ((s8[14155776]{0:T(1024)(128)(4,1)}), s8[1572864]{0:T(1024)(128)(4,1)S(1)}, s32[]{:S(2)}) async-start(s8[14155776]{0:T(1024)(128)(4,1)} %bitcast.114), calls=%async_computation.6 | async-start | bytes 3145728
  737.5 8.7 %copy-start.4 = (pred[24,384]{1,0:T(8,128)(4,1)S(1)}, pred[24,384]{1,0:T(8,128)(4,1)}, u32[]{:S(2)}) copy-start(pred[24,384]{1,0:T(8,128)(4,1)} %copy-done.3) | copy-start | bytes 27652
  746.3 32.0 %copy-start.1 = (bf16[512,256]{1,0:T(8,128)(2,1)S(1)}, bf16[512,256]{1,0:T(8,128)(2,1)}, u32[]{:S(2)}) copy-start(bf16[512,256]{1,0:T(8,128)(2,1)} %param.10) | copy-start | bytes 786436
Sparse Core Ops, SparseCore 0:
  247.8 152.7 all-gather.1
where the time goes:
time: 794 us; the launch traced here: 786 us
  waiting for transfers between devices  321 us (40%)
  blocking collectives  211 us (27%)
  matrix products  120 us (15%)
  local copies, waits for them, and re-layouts  95.2 us (12%)
  between operations  14.1 us (2%)
  starting transfers between devices  13.5 us (2%)
  other arithmetic  10.8 us (1%)
    all_to_all x1, blocking collectives, on_device(): lax.all_to_all(modes, 'lat', split_axis=0, concat_axis=4, tiled=True)  211 us
    all_to_all x1, waiting for transfers between devices, on_device(): lax.all_to_all(coeff, 'lat', split_axis=4, concat_axis=0, tiled=True)  165 us
    all_gather x1, waiting for transfers between devices, on_device(): whole = lax.all_gather(grid, 'chan', axis=2, tiled=True)  153 us
    dot_general x1, matrix products, on_device(): modes = jnp.einsum('btcp,srp->sbcrt', field, waves, precision=high)  41.4 us
    slice x1, local copies, waits for them, and re-layouts, on_device(): jnp.roll(band, 1 - j, axis=3)  38.6 us
    dot_general x1, matrix products, on_device(): jnp.einsum('sbcrt,srp->btcp', lax.all_to_all(coeff, 'lat', split_axis=4,...  24.7 us
    dot_general x1, matrix products, on_device(): jnp.einsum('sbcrt,stl->sbcrl', lax.all_to_all(modes, 'lat', split_axis=0,...  22.6 us
    dot_general x1, local copies, waits for them, and re-layouts, on_device(): jnp.einsum('sbcrl,stl->sbcrt', spec_in.astype(jnp.float32), masked, preci...  21.3 us
  transfers between devices with their start and end apart: 4, of which 3 were waited for; matrix products, arithmetic and copies ran while one was open for 1% of the time, Pallas kernels for 0%

commit v1 on v0

--- a/solution.py
+++ b/solution.py
@@ -1,8 +1,11 @@
+import functools
 import math
 
 import jax
 import jax.numpy as jnp
 from jax import lax
+from jax.experimental import pallas as pl
+from jax.experimental.pallas import tpu as pltpu
 from jax.sharding import PartitionSpec as P
 
 NLON = 768
@@ -76,6 +79,136 @@
     ).astype(jnp.bfloat16)
 
 
+def all_taps(taps, axis):
+    count, index, width = lax.axis_size(axis), lax.axis_index(axis), taps.shape[1]
+    ring = [(i, (i + 1) % count) for i in range(count)]
+    whole = jnp.zeros((taps.shape[0], count * width), taps.dtype)
+    for step in range(count):
+        owner = (index - step) % count
+        whole = lax.dynamic_update_slice_in_dim(whole, taps, owner * width, 1)
+        if step < count - 1:
+            taps = lax.ppermute(taps, axis, ring)
+    return whole
+
+
+def conv_halo(mixed, axes):
+    count, index = lax.axis_size(axes), lax.axis_index(axes)
+    half = mixed.shape[1] // 2
+    up = [(i, i + 1) for i in range(count - 1)]
+    down = [(j, i) for i, j in up]
+    before = lax.ppermute(mixed[-1], axes, up)
+    after = lax.ppermute(mixed[0], axes, down)
+    before = jnp.where(index == 0, jnp.roll(mixed[0], half, axis=0), before)
+    after = jnp.where(index == count - 1, jnp.roll(mixed[-1], half, axis=0), after)
+    return before, after
+
+
+def grid_kernel(lats, chans, coeff_ref, waves_ref, w_in_ref, b_in_ref, w_out_ref, mixed_ref):
+    rows, width = coeff_ref.shape[2], coeff_ref.shape[3]
+    coeff = coeff_ref[...].reshape(lats, chans, rows, width)
+    parts = [coeff[:, j].reshape(lats * rows, width) for j in range(chans)]
+    merged = jnp.concatenate(parts, axis=1)
+    grid = jnp.dot(waves_ref[...], merged, preferred_element_type=jnp.float32).astype(jnp.bfloat16)
+    pre = jnp.dot(grid, w_in_ref[...], preferred_element_type=jnp.float32) + b_in_ref[...]
+    hidden = jax.nn.gelu(pre, approximate=True).astype(jnp.bfloat16)
+    branch = jnp.dot(hidden, w_out_ref[...], preferred_element_type=jnp.float32)
+    mixed_ref[0] = (grid.astype(jnp.float32) + branch).astype(jnp.bfloat16)
+
+
+def field_kernel(lats, chans, here_ref, prev_ref, next_ref, before_ref, after_ref, kernel_ref, waves_ref, modes_ref):
+    row, last = pl.program_id(0), pl.num_programs(0) - 1
+    here = here_ref[0].astype(jnp.float32)
+    prev = jnp.where(row == 0, before_ref[...].astype(jnp.float32), prev_ref[0].astype(jnp.float32))
+    after = jnp.where(row == last, after_ref[...].astype(jnp.float32), next_ref[0].astype(jnp.float32))
+    count = here.shape[0]
+    taps = [
+        kernel_ref[j : j + 1] * prev + kernel_ref[3 + j : 4 + j] * here + kernel_ref[6 + j : 7 + j] * after
+        for j in range(3)
+    ]
+    field = here + taps[1] + pltpu.roll(taps[0], 1, 0) + pltpu.roll(taps[2], count - 1, 0)
+    modes = jnp.dot(waves_ref[...], field.astype(jnp.bfloat16), preferred_element_type=jnp.float32)
+    modes = modes.astype(jnp.bfloat16)
+    rows, width = modes_ref.shape[2], modes_ref.shape[3]
+    for i in range(lats):
+        for j in range(chans):
+            modes_ref[i * chans + j, 0] = modes[i * rows : (i + 1) * rows, j * width : (j + 1) * width]
+
+
+def on_device_rows(spec_in, legendre, mode_slot, w_in, b_in, w_out, kernel):
+    axes = ("lat", "chan")
+    lats, chans = lax.axis_size("lat"), lax.axis_size("chan")
+    count = lats * chans
+    slots, rows_all, degrees_all = legendre.shape
+    width = spec_in.shape[2]
+    rows = rows_all // count
+    columns = NLON
+    channels = width * chans
+    lat_index = lax.axis_index("lat")
+    local_modes = lax.dynamic_slice_in_dim(mode_slot, lat_index * slots, slots)
+    degrees = jnp.arange(degrees_all, dtype=jnp.int32)
+    keep = degrees[None, None, :] >= local_modes[:, None, None]
+    masked = jnp.where(keep, legendre, jnp.float32(0.0)).astype(jnp.bfloat16)
+    waves = wave_table(mode_slot, columns).astype(jnp.bfloat16)
+    waves = jnp.swapaxes(waves.reshape(lats, slots, 2, columns), 1, 2).reshape(-1, columns)
+    taps = all_taps(kernel.T, "chan")
+    coeff = jnp.einsum("scrl,stl->trsc", spec_in[:, 0], masked, preferred_element_type=jnp.float32)
+    coeff = coeff.astype(jnp.bfloat16).reshape(rows_all, 2 * slots, width)
+    coeff = lax.all_to_all(coeff, axes, split_axis=0, concat_axis=0, tiled=True)
+    coeff = coeff.reshape(count, rows, 2 * slots, width)
+    packed = pl.BlockSpec((count, 1, 2 * slots, width), lambda t: (0, t, 0, 0))
+
+    def whole(array):
+        return pl.BlockSpec(array.shape, lambda t: (0,) * array.ndim)
+
+    w_in_t, w_out_t, bias, waves_t = w_in.T, w_out.T, b_in[None, :], waves.T
+    params = pltpu.CompilerParams(vmem_limit_bytes=48 * 1024 * 1024)
+
+    def mixed_rows(steps, stride, name):
+        work = columns * channels * (waves_t.shape[1] + 2 * w_in_t.shape[1])
+        return pl.pallas_call(
+            functools.partial(grid_kernel, lats, chans),
+            grid=(steps,),
+            out_shape=jax.ShapeDtypeStruct((steps, columns, channels), jnp.bfloat16),
+            in_specs=[
+                pl.BlockSpec((count, 1, 2 * slots, width), lambda t: (0, t * stride, 0, 0)),
+                whole(waves_t), whole(w_in_t), whole(bias), whole(w_out_t),
+            ],
+            out_specs=pl.BlockSpec((1, columns, channels), lambda t: (t, 0, 0)),
+            compiler_params=params,
+            cost_estimate=pl.CostEstimate(
+                flops=2 * steps * work, bytes_accessed=coeff.nbytes, transcendentals=0
+            ),
+            name=name,
+        )(coeff, waves_t, w_in_t, bias, w_out_t)
+
+    edges = mixed_rows(min(2, rows), max(rows - 1, 1), "grid_edges")
+    before, after = conv_halo(edges, axes)
+    mixed = mixed_rows(rows, 1, "grid_mlp")
+    line = (1, columns, channels)
+    modes = pl.pallas_call(
+        functools.partial(field_kernel, lats, chans),
+        grid=(rows,),
+        out_shape=jax.ShapeDtypeStruct((count, rows, 2 * slots, width), jnp.bfloat16),
+        in_specs=[
+            pl.BlockSpec(line, lambda t: (t, 0, 0)),
+            pl.BlockSpec(line, lambda t: (jnp.maximum(t - 1, 0), 0, 0)),
+            pl.BlockSpec(line, lambda t: (jnp.minimum(t + 1, rows - 1), 0, 0)),
+            whole(before),
+            whole(after),
+            whole(taps),
+            whole(waves),
+        ],
+        out_specs=packed,
+        compiler_params=params,
+        name="conv_dft",
+    )(mixed, mixed, mixed, before, after, taps, waves)
+    modes = modes.reshape(rows_all, 2 * slots, width)
+    modes = lax.all_to_all(modes, axes, split_axis=0, concat_axis=0, tiled=True)
+    modes = modes.reshape(rows_all, 2, slots, width)
+    out = jnp.einsum("trsc,stl->scrl", modes, masked, preferred_element_type=jnp.float32)
+    return out.astype(jnp.bfloat16)[:, None]
+
+
 def solution(mesh):
     in_specs = (
         P("lat", None, "chan", None, None),
@@ -87,6 +220,14 @@
         P("chan", None),
     )
     out_specs = P("lat", None, "chan", None, None)
-    return jax.shard_map(
-        on_device, mesh=mesh, in_specs=in_specs, out_specs=out_specs, check_vma=False
-    )
+    count = mesh.shape["lat"] * mesh.shape["chan"]
+
+    def call(spec_in, legendre, *rest):
+        samples, rows_all = spec_in.shape[1], legendre.shape[1]
+        by_rows = samples == 1 and rows_all % count == 0
+        body = on_device_rows if by_rows else on_device
+        return jax.shard_map(
+            body, mesh=mesh, in_specs=in_specs, out_specs=out_specs, check_vma=False
+        )(spec_in, legendre, *rest)
+
+    return call

time: 794 us -> 320 us (0.40)
  waiting for transfers between devices: 321 us -> 106 us
  blocking collectives: 211 us -> 111 us
  matrix products: 120 us -> 20.3 us
  local copies, waits for them, and re-layouts: 95.2 us -> 19.5 us
  Pallas kernels: 0 us -> 42.6 us
  between operations: 14.1 us -> 0.24 us
    all_gather x1 -> x0, waiting for transfers between devices: 153 us -> none  [on_device(): whole = lax.all_gather(grid, 'chan', axis=2, tiled=True)]
    all_to_all x1, blocking collectives: 211 us -> 111 us  [on_device_rows(): modes = lax.all_to_all(modes, axes, split_axis=0, concat_axis=0, tiled=True)]
    dot_general x5 -> x2, matrix products: 120 us -> 20.3 us  [the longest x1 12 us: on_device_rows(): jnp.einsum('trsc,stl->scrl', modes, masked, preferred_element_type=jnp.fl...]
    all_to_all x1, waiting for transfers between devices: 165 us -> 81.1 us  [on_device_rows(): coeff = lax.all_to_all(coeff, axes, split_axis=0, concat_axis=0, tiled=True)]
    pallas_call x0 -> x3, Pallas kernels: none -> 42.6 us  [the longest x2 25.3 us: mixed_rows(): pl.pallas_call(functools.partial(grid_kernel, lats, chans), grid=(steps,)...]
    slice x3 -> x1, local copies, waits for them, and re-layouts: 40.8 us -> 0.05 us  [conv_halo(): jnp.roll(mixed[-1], half, axis=0)]
    dot_general x1 -> x0, local copies, waits for them, and re-layouts: 21.3 us -> none  [on_device(): jnp.einsum('sbcrl,stl->sbcrt', spec_in.astype(jnp.float32), masked, preci...]
    ppermute x2 -> x3, waiting for transfers between devices: 3.75 us -> 25 us  [the longest x1 15.8 us: all_taps(): taps = lax.ppermute(taps, axis, ring)]
  transfers between devices with their start and end apart: 4 -> 4, of which waited for: 3 -> 3; matrix products, arithmetic and copies ran while one was open for 1% -> 2% of each run, Pallas kernels for 0% -> 7%
where the time goes in v1:
time: 320 us; the launch traced here: 319 us
  blocking collectives  111 us (35%)
  waiting for transfers between devices  106 us (33%)
  Pallas kernels  42.6 us (13%)
  matrix products  20.3 us (6%)
  local copies, waits for them, and re-layouts  19.5 us (6%)
  starting transfers between devices  14.1 us (4%)
  other arithmetic  5.81 us (2%)
    all_to_all x1, blocking collectives, on_device_rows(): modes = lax.all_to_all(modes, axes, split_axis=0, concat_axis=0, tiled=True)  111 us
    all_to_all x1, waiting for transfers between devices, on_device_rows(): coeff = lax.all_to_all(coeff, axes, split_axis=0, concat_axis=0, tiled=True)  81.1 us
    pallas_call x2, Pallas kernels, mixed_rows(): pl.pallas_call(functools.partial(grid_kernel, lats, chans), grid=(steps,)...  25.3 us
    pallas_call x1, Pallas kernels, on_device_rows(): pl.pallas_call(functools.partial(field_kernel, lats, chans), grid=(rows,)...  17.3 us
    ppermute x1, waiting for transfers between devices, all_taps(): taps = lax.ppermute(taps, axis, ring)  15.8 us
    broadcast_in_dim x1, local copies, waits for them, and re-layouts, on_device_rows(): return out.astype(jnp.bfloat16)[:, None]  12.4 us
    dot_general x1, matrix products, on_device_rows(): jnp.einsum('trsc,stl->scrl', modes, masked, preferred_element_type=jnp.fl...  12 us
    ppermute x1, waiting for transfers between devices, conv_halo(): after = lax.ppermute(mixed[0], axes, down)  9.16 us
  transfers between devices with their start and end apart: 4, of which 3 were waited for; matrix products, arithmetic and copies ran while one was open for 2% of the time, Pallas kernels for 7%

profile of v1, /device:TPU:1, one launch (start us, length us, event | category | flops | bytes accessed | tf_op | source)
XLA Modules:
  0.0 319.2 jit_solution(7115556850699575564)
XLA Ops:
  0.0 0.8 dynamic_slice.3
  0.8 0.1 iota_compare_fusion
  0.8 8.3 %convert_bitcast_fusion.1 = bf16[384,2,24,128]{3,0,1,2:T(8,128)(2,1)S(1)} fusion(bf16[24,128,2,384]{3,2,1,0:T(2,128)(2,1)} %bitcast.53, f32[24,384,384]{2,1,0:T(8,128)} %param.8, pred[24,384]{1,0:T(8,128)(4,1)S(1)} %iota_compare_fusion), kind=kOutput, calls=%fused_computation.7 | convolution fusion | flops 1817837568 | bytes 23602176 | tf_op jit(solution)/shard_map/scrl,stl->trsc/dot_general | solution.py:154
  9.2 5.2 %copy.16 = bf16[384,2,24,128]{3,2,1,0:T(8,128)(2,1)} copy(bf16[384,2,24,128]{3,0,1,2:T(8,128)(2,1)S(1)} %convert_bitcast_fusion.1) | data formatting | bytes 9437184 | tf_op jit(solution)/shard_map/convert_element_type | solution.py:155
  14.4 7.1 %all-to-all-start = ((bf16[384,48,128]{2,1,0:T(8,128)(2,1)}), bf16[384,48,128]{2,1,0:T(8,128)(2,1)}, u32[]{:S(2)}, u32[]{:S(2)}) async-start(bf16[384,48,128]{2,1,0:T(8,128)(2,1)} %bitcast.50), calls=%async_computation | async-start | bytes 9437184 | tf_op jit(solution)/shard_map/all_to_all | solution.py:156
  21.6 0.0 copy-start.1
  21.6 0.0 copy-start.2
  21.6 0.0 copy-start
  21.6 1.4 collective-permute-start.2
  23.0 0.0 copy-done.4
  23.0 0.1 mul.82
  23.2 5.4 %multiply_convert_fusion.1 = (bf16[16,24,1,768]{3,1,2,0:T(8,128)(2,1)S(1)}, bf16[16,24,1,768]{3,1,2,0:T(8,128)(2,1)S(1)}) fusion(s32[16,24]{1,0:T(8,128)S(1)} %mul.82), kind=kLoop, calls=%fused_computation.13 | loop fusion | flops 4128768 | bytes 1181184 | tf_op jit(solution)/shard_map/convert | solution.py:229
  28.6 0.1 pad_maximum_fusion
  28.7 0.6 copy.19.waves_ref
  29.4 0.1 copy.17
  29.5 0.1 copy.18
  29.7 15.8 %collective-permute-done.2 = f32[9,128]{1,0:T(8,128)S(1)} collective-permute-done((f32[9,128]{1,0:T(8,128)S(1)}, f32[9,128]{1,0:T(8,128)S(1)}, u32[]{:S(2)}, u32[]{:S(2)}) %collective-permute-start.2) | collective-permute-done | bytes 4640 | tf_op jit(solution)/shard_map/ppermute | solution.py:90
  45.5 81.1 %all-to-all-done = bf16[384,48,128]{2,1,0:T(8,128)(2,1)} async-done(((bf16[384,48,128]{2,1,0:T(8,128)(2,1)}), bf16[384,48,128]{2,1,0:T(8,128)(2,1)}, u32[]{:S(2)}, u32[]{:S(2)}) %all-to-all-start) | async-done | bytes 4718624 | tf_op jit(solution)/shard_map/all_to_all | solution.py:156
  126.6 4.2 %grid_edges.1 = bf16[2,768,256]{2,1,0:T(8,128)(2,1)S(1)} custom-call(bf16[32,12,48,128]{3,2,1,0:T(8,128)(2,1)} %bitcast.6.coeff_ref, bf16[768,768]{1,0:T(8,128)(2,1)S(1)} %copy.19.waves_ref, bf16[256,512]{1,0:T(8,128)(2,1)S(1)} %bitcast.44, f32[1,512]{1,0:T(1,128)S(1)} %bitcast.48, bf16[512,256]{1,0:T(8,128)(2,1)S(1)} %bitcast.46), custom_call_target="tpu_custom_call" | custom-call | flops 1409286144 | bytes 4718592 | tf_op jit(solution)/shard_map/grid_edges/pallas_call | solution.py:168
  130.8 0.1 slice_bitcast_fusion
  130.9 2.3 collective-permute-start
  133.2 21.1 %grid_mlp.1.here_ref.prev_ref.next_ref = bf16[12,768,256]{2,1,0:T(8,128)(2,1)} custom-call(bf16[32,12,48,128]{3,2,1,0:T(8,128)(2,1)} %bitcast.6.coeff_ref, bf16[768,768]{1,0:T(8,128)(2,1)S(1)} %copy.19.waves_ref, bf16[256,512]{1,0:T(8,128)(2,1)S(1)} %bitcast.45, f32[1,512]{1,0:T(1,128)S(1)} %bitcast.49, bf16[512,256]{1,0:T(8,128)(2,1)S(1)} %bitcast.47), custom_call_target="tpu_custom_call" | custom-call | flops 8455716864 | bytes 4718592 | tf_op jit(solution)/shard_map/grid_mlp/pallas_call | solution.py:168
  154.3 3.2 %collective-permute-start.1 = (bf16[768,256]{1,0:T(8,128)(2,1)S(1)}, bf16[768,256]{1,0:T(8,128)(2,1)S(1)}, u32[]{:S(2)}, u32[]{:S(2)}) collective-permute-start(bf16[768,256]{1,0:T(8,128)(2,1)S(1)} %get-tuple-element.9), channel_id=1, source_target_pairs={{1,0},{2,1},{3,2},{4,3},{5,4},{6,5},{7,6},{8,7},{9,8},{10,9},{11,1... | collective-permute-start | bytes 1179656 | tf_op jit(solution)/shard_map/ppermute | solution.py:100
  157.5 0.1 slice_bitcast_fusion.3
  157.6 0.0 collective-permute-done
  157.6 0.1 maximum_select_fusion.before_ref
  157.7 9.2 %collective-permute-done.1 = bf16[768,256]{1,0:T(8,128)(2,1)S(1)} collective-permute-done((bf16[768,256]{1,0:T(8,128)(2,1)S(1)}, bf16[768,256]{1,0:T(8,128)(2,1)S(1)}, u32[]{:S(2)}, u32[]{:S(2)}) %collective-permute-start.1) | collective-permute-done | bytes 393248 | tf_op jit(solution)/shard_map/ppermute | solution.py:100
  166.9 0.1 maximum_select_fusion.1.after_ref
  167.0 17.3 %conv_dft.1 = bf16[32,12,48,128]{3,2,1,0:T(8,128)(2,1)} custom-call(bf16[12,768,256]{2,1,0:T(8,128)(2,1)} %grid_mlp.1.here_ref.prev_ref.next_ref, bf16[12,768,256]{2,1,0:T(8,128)(2,1)} %grid_mlp.1.here_ref.prev_ref.next_ref, bf16[12,768,256]{2,1,0:T(8,128)(2,1)} %grid_mlp.1.here_ref.prev_ref.next_ref, bf16[768,256]{1,0:T(8,128)(2,1)S(1)} %maximum_select_fusion.before_ref, ...), custom_call_target="tpu_custom_call" | custom-call | tf_op jit(solution)/shard_map/conv_dft/pallas_call | solution.py:188
  184.3 110.5 %all_to_all.10 = bf16[384,48,128]{2,1,0:T(8,128)(2,1)} all-to-all(bf16[384,48,128]{2,1,0:T(8,128)(2,1)} %bitcast.51), channel_id=1, replica_groups=mesh['lat'=16,'chan'=2] {'lat','chan'}, dimensions={0} | all-to-all | bytes 9437184 | tf_op jit(solution)/shard_map/all_to_all | solution.py:206
  294.8 12.0 %convert_bitcast_fusion = bf16[24,1,128,2,384]{2,4,3,0,1:T(8,128)(2,1)} fusion(bf16[384,2,24,128]{3,2,1,0:T(8,128)(2,1)} %bitcast.52, f32[24,384,384]{2,1,0:T(8,128)} %param.8, pred[24,384]{1,0:T(8,128)(4,1)S(1)} %iota_compare_fusion), kind=kOutput, calls=%fused_computation.6 | convolution fusion | flops 1817837568 | bytes 23602176 | tf_op jit(solution)/shard_map/trsc,stl->scrl/dot_general | solution.py:208
  306.8 12.4 %copy.23 = bf16[24,1,128,2,384]{4,3,2,1,0:T(2,128)(2,1)} copy(bf16[24,1,128,2,384]{2,4,3,0,1:T(8,128)(2,1)} %convert_bitcast_fusion) | data formatting | bytes 9437184 | tf_op jit(solution)/shard_map/broadcast_in_dim | solution.py:209
  (9 shorter events, 0.0 us)
Async XLA Ops:
  14.4 7.2 %copy-start.3 = (f32[128,9]{0,1:T(8,128)S(1)}, f32[128,9]{0,1:T(8,128)}, u32[]{:S(2)}) copy-start(f32[128,9]{0,1:T(8,128)} %param.13) | copy-start | bytes 13828
  14.4 8.6 %copy-start.4 = (s32[384]{0:T(512)S(1)}, s32[384]{0:T(512)}, u32[]{:S(2)}) copy-start(s32[384]{0:T(512)} %param.9) | copy-start | bytes 4612
  14.4 112.2 %all-to-all-start = ((bf16[384,48,128]{2,1,0:T(8,128)(2,1)}), bf16[384,48,128]{2,1,0:T(8,128)(2,1)}, u32[]{:S(2)}, u32[]{:S(2)}) async-start(bf16[384,48,128]{2,1,0:T(8,128)(2,1)} %bitcast.50), calls=%async_computation | async-start | bytes 9437184 | tf_op jit(solution)/shard_map/all_to_all | solution.py:156
  21.6 7.8 %copy-start.1 = (bf16[512,256]{1,0:T(8,128)(2,1)S(1)}, bf16[512,256]{1,0:T(8,128)(2,1)}, u32[]{:S(2)}) copy-start(bf16[512,256]{1,0:T(8,128)(2,1)} %param.10) | copy-start | bytes 786436
  21.6 8.0 %copy-start.2 = (bf16[256,512]{1,0:T(8,128)(2,1)S(1)}, bf16[256,512]{1,0:T(8,128)(2,1)}, u32[]{:S(2)}) copy-start(bf16[256,512]{1,0:T(8,128)(2,1)} %param.12) | copy-start | bytes 786436
  21.6 105.0 %copy-start = (f32[512]{0:T(512)S(1)}, f32[512]{0:T(512)}, u32[]{:S(2)}) copy-start(f32[512]{0:T(512)} %param.11) | copy-start | bytes 6148
  21.6 23.9 %collective-permute-start.2 = (f32[9,128]{1,0:T(8,128)S(1)}, f32[9,128]{1,0:T(8,128)S(1)}, u32[]{:S(2)}, u32[]{:S(2)}) collective-permute-start(f32[9,128]{1,0:T(8,128)S(1)} %bitcast.54), channel_id=1, source_target_pairs={{0,1},{1,0},{2,3},{3,2},{4,5},{5,4},{6,7},{7,6},{8,9},{9,8},{10,11... | collective-permute-start | bytes 13832 | tf_op jit(solution)/shard_map/ppermute | solution.py:90
  130.9 26.7 %collective-permute-start = (bf16[768,256]{1,0:T(8,128)(2,1)S(1)}, bf16[768,256]{1,0:T(8,128)(2,1)S(1)}, u32[]{:S(2)}, u32[]{:S(2)}) collective-permute-start(bf16[768,256]{1,0:T(8,128)(2,1)S(1)} %get-tuple-element.10), channel_id=1, source_target_pairs={{0,1},{1,2},{2,3},{3,4},{4,5},{5,6},{6,7},{7,8},{8,9},{9,10},{10,1... | collective-permute-start | bytes 1179656 | tf_op jit(solution)/shard_map/ppermute | solution.py:99
  154.3 12.6 %collective-permute-start.1 = (bf16[768,256]{1,0:T(8,128)(2,1)S(1)}, bf16[768,256]{1,0:T(8,128)(2,1)S(1)}, u32[]{:S(2)}, u32[]{:S(2)}) collective-permute-start(bf16[768,256]{1,0:T(8,128)(2,1)S(1)} %get-tuple-element.9), channel_id=1, source_target_pairs={{1,0},{2,1},{3,2},{4,3},{5,4},{6,5},{7,6},{8,7},{9,8},{10,9},{11,1... | collective-permute-start | bytes 1179656 | tf_op jit(solution)/shard_map/ppermute | solution.py:100
